TPU v7x, 32 devices: a 4x2x2 block of a 4x4x8 slice. The times are simulated.
32 devices in a mesh: data: 4 (over y, z), tp: 8 (over x, core).
Axes of the slice: x: 4, y: 2, z: 2, core: 2. Of those that a mesh axis runs over, the one named last changes fastest.
The devices are a block of a 4x4x8 slice.
Arguments:
- x_in: bfloat16 [32768, 1536], P('data'), parts along dimension 0
- w_gate: bfloat16 [1536, 8960], P(None, 'tp')
- w_up: bfloat16 [1536, 8960], P(None, 'tp')
- w_down: bfloat16 [8960, 1536], P('tp')
- residual: bfloat16 [32768, 1536], P(('data', 'tp')), parts along dimension 0
- norm_gain: float32 [1536], replicated
Outputs:
- output 1: bfloat16 [32768, 1536], P(('data', 'tp')), parts along dimension 0
- output 2: bfloat16 [32768, 1536], P(('data', 'tp')), parts along dimension 0
There are 4 independent parts. A program takes and returns all parts, laid end to end along the dimension named above; an argument that names none is the same for every part.
All inputs are finite; a program needn't handle non-finite values.
Results may differ from a plain program's by a relative error of at most 0.00648195.
Values are sent between devices in bfloat16 or wider.
A program may use at most 768 MiB of HBM per device.

v0:
```python
import jax
import jax.numpy as jnp
from jax import lax
from jax.sharding import PartitionSpec as P

EPS = 1e-5


def add_and_norm(y_sum, residual, norm_gain):
    hidden_sum = residual.astype(jnp.float32) + y_sum
    mean_sq = jnp.mean(hidden_sum * hidden_sum, axis=-1, keepdims=True)
    normed = hidden_sum * lax.rsqrt(mean_sq + EPS) * norm_gain
    return hidden_sum.astype(jnp.bfloat16), normed.astype(jnp.bfloat16)


def solution(mesh):
    tp_size = mesh.shape["tp"]

    def local_block(x_in, w_gate, w_up, w_down, residual, norm_gain):
        gate_val = jnp.dot(x_in, w_gate, preferred_element_type=jnp.float32)
        up_val = jnp.dot(x_in, w_up, preferred_element_type=jnp.float32)
        hidden = (jax.nn.silu(gate_val) * up_val).astype(jnp.bfloat16)
        part_prod = jnp.dot(hidden, w_down, preferred_element_type=jnp.float32).astype(jnp.bfloat16)
        received = lax.all_to_all(part_prod, "tp", 0, 0, tiled=True)
        rows = residual.shape[0]
        y_sum = jnp.sum(received.reshape(tp_size, rows, received.shape[1]), axis=0, dtype=jnp.float32)
        return add_and_norm(y_sum, residual, norm_gain)

    row_spec = P(("data", "tp"), None)
    return jax.shard_map(local_block, mesh=mesh, in_specs=(P("data", None), P(None, "tp"), P(None, "tp"), P("tp", None), row_spec, P(None)), out_specs=(row_spec, row_spec), check_vma=False)
```

profile of v0, /device:TPU:81, one launch (start us, length us, event | category | flops | bytes accessed | tf_op | source)
XLA Modules:
  0.0 427.4 jit_solution(6187483761194141759)
XLA Ops:
  0.6 0.0 copy-start
  0.6 36.8 %fusion.3 = f32[8192,1120]{0,1:T(8,128)} fusion(bf16[8192,1536]{1,0:T(8,128)(2,1)} %param.6, bf16[1536,1120]{0,1:T(8,128)(2,1)} %param.7), kind=kOutput, calls=%fused_computation.10 | convolution fusion | flops 28185722880 | bytes 65306624 | tf_op jit(solution)/shard_map/dot_general | solution.py:20
  37.4 40.3 %fusion.clone.4 = bf16[8192,1120]{0,1:T(8,128)(2,1)} fusion(bf16[8192,1536]{1,0:T(8,128)(2,1)} %param.6, bf16[1536,1120]{0,1:T(8,128)(2,1)} %param.8, f32[8192,1120]{0,1:T(8,128)} %fusion.3), kind=kOutput, calls=%fused_computation.2.clone.clone.clone.1 | convolution fusion | flops 28240773120 | bytes 83656704 | tf_op jit(solution)/shard_map/dot_general | solution.py:21
  77.7 0.0 copy-done
  77.7 38.7 %convolution_convert_fusion = bf16[8192,1536]{1,0:T(8,128)(2,1)} fusion(bf16[1120,1536]{1,0:T(8,128)(2,1)S(1)} %copy-done, bf16[8192,1120]{0,1:T(8,128)(2,1)} %fusion.clone.4), kind=kOutput, calls=%fused_computation.3 | convolution fusion | flops 28198305792 | bytes 46956544 | tf_op jit(solution)/shard_map/dot_general | solution.py:23
  116.4 284.6 %all_to_all.9 = bf16[8,1024,1536]{2,1,0:T(8,128)(2,1)} all-to-all(bf16[8,1024,1536]{2,1,0:T(8,128)(2,1)} %bitcast.14), channel_id=1, replica_groups=mesh['data'=4,'tp'=8] {'tp'}, dimensions={0} | all-to-all | bytes 50331648 | tf_op jit(solution)/shard_map/all_to_all | solution.py:24
  401.1 16.2 %convert_reduce_fusion = f32[1024,1536]{1,0:T(8,128)} fusion(bf16[8,1024,1536]{2,1,0:T(8,128)(2,1)} %all_to_all.9), kind=kLoop, calls=%fused_computation | loop fusion | flops 23592960 | bytes 31457280 | tf_op jit(solution)/shard_map/reduce_sum | solution.py:26
  417.2 0.0 copy-start.1
  417.2 0.0 copy-start.2
  417.2 0.0 copy-start.3
  417.2 4.7 %multiply_reduce_fusion = f32[1024]{0:T(1024)S(1)} fusion(f32[1024,1536]{1,0:T(8,128)} %convert_reduce_fusion, bf16[1024,1536]{1,0:T(8,128)(2,1)} %param.10), kind=kLoop, calls=%fused_computation.5 | loop fusion | flops 6290432 | bytes 9441280 | tf_op jit(solution)/shard_map/reduce_sum | solution.py:11
  422.0 0.7 copy-done.1
  422.7 0.9 copy-done.2
  423.7 0.0 copy-done.3
  423.7 3.7 multiply_convert_fusion
  (1 shorter events, 0.0 us)
Async XLA Ops:
  0.6 77.1 %copy-start = (bf16[1120,1536]{1,0:T(8,128)(2,1)S(1)}, bf16[1120,1536]{1,0:T(8,128)(2,1)}, u32[]{:S(2)}) copy-start(bf16[1120,1536]{1,0:T(8,128)(2,1)} %param.9) | copy-start | bytes 10321924
  417.2 5.5 %copy-start.1 = (f32[1024,1536]{1,0:T(8,128)S(1)}, f32[1024,1536]{1,0:T(8,128)}, u32[]{:S(2)}) copy-start(f32[1024,1536]{1,0:T(8,128)} %convert_reduce_fusion) | copy-start | bytes 18874372
  417.2 6.4 %copy-start.2 = (bf16[1024,1536]{1,0:T(8,128)(2,1)S(1)}, bf16[1024,1536]{1,0:T(8,128)(2,1)}, u32[]{:S(2)}) copy-start(bf16[1024,1536]{1,0:T(8,128)(2,1)} %param.10) | copy-start | bytes 9437188
  417.2 6.4 %copy-start.3 = (f32[1536]{0:T(1024)S(1)}, f32[1536]{0:T(1024)}, u32[]{:S(2)}) copy-start(f32[1536]{0:T(1024)} %param.11) | copy-start | bytes 18436
where the time goes:
time: 428 us; the launch traced here: 427 us
  blocking collectives  285 us (67%)
  matrix products  116 us (27%)
  other arithmetic  24.7 us (6%)
    all_to_all x1, blocking collectives, local_block(): received = lax.all_to_all(part_prod, 'tp', 0, 0, tiled=True)  285 us
    dot_general x1, matrix products, local_block(): up_val = jnp.dot(x_in, w_up, preferred_element_type=jnp.float32)  40.3 us
    dot_general x1, matrix products, local_block(): jnp.dot(hidden, w_down, preferred_element_type=jnp.float32)  38.7 us
    dot_general x1, matrix products, local_block(): gate_val = jnp.dot(x_in, w_gate, preferred_element_type=jnp.float32)  36.8 us
    reduce_sum x1, other arithmetic, local_block(): jnp.sum(received.reshape(tp_size, rows, received.shape[1]), axis=0, dtype...  16.2 us

commit v1 on v0

v1 whole, which is shorter than its diff:
```python
import functools

import jax
import jax.numpy as jnp
from jax import lax
from jax.experimental import pallas as pl
from jax.experimental.pallas import tpu as pltpu
from jax.sharding import PartitionSpec as P

EPS = 1e-5
MESH = pl.DeviceIdType.MESH
TILE = 256
LANE = 128


def dot_nt(a, b):
    return lax.dot_general(a, b, (((1,), (1,)), ((), ())), preferred_element_type=jnp.float32)


def mlp_kernel(
    tp, x_hbm, wg_hbm, wu_hbm, wd_hbm, res_hbm, gain_ref, h_ref, n_ref,
    wg, wu, wt, wd, xbuf, gbuf, dsend, drecv, rrecv, res, hsum,
    w_sem, x_sem, res_sem, ds_sem, dr_sem, rs_sem, rr_sem,
):
    rows = res_hbm.shape[0]
    width = res_hbm.shape[1]
    hid = wg_hbm.shape[0]
    main = hid // LANE * LANE
    tail = hid - main
    chips = tp // 2
    subs = rows // TILE
    sends = (chips - 1) * subs
    total = chips * subs

    me = lax.axis_index("tp")
    chip, core = me // 2, lax.rem(me, 2)
    step_dir = 1 - 2 * core
    partner = me + step_dir
    ahead = 2 * lax.rem(chip + step_dir + chips, chips) + core
    behind = 2 * lax.rem(chip - step_dir + chips, chips) + core

    def my_dest(s):
        return 2 * lax.rem(chip - s * step_dir + 2 * chips, chips) + core

    def partner_dest(s):
        return 2 * lax.rem(chip + s * step_dir + 2 * chips, chips) + (1 - core)

    def x_copy(t, which, slot):
        s, j = t // subs + 1, lax.rem(t, subs)
        dest = my_dest(s) if which else partner_dest(s)
        start = pl.multiple_of(dest * rows + j * TILE, TILE)
        return pltpu.make_async_copy(x_hbm.at[pl.ds(start, TILE), :], xbuf.at[slot, which], x_sem.at[slot, which])

    x_copy(0, 0, 0).start()
    w_copies = [
        pltpu.make_async_copy(wg_hbm.at[pl.ds(0, main), :], wg, w_sem.at[0]),
        pltpu.make_async_copy(wu_hbm.at[pl.ds(0, main), :], wu, w_sem.at[1]),
        pltpu.make_async_copy(wg_hbm.at[pl.ds(main, tail), :], wt.at[pl.ds(0, tail), :], w_sem.at[2]),
        pltpu.make_async_copy(wu_hbm.at[pl.ds(main, tail), :], wt.at[pl.ds(LANE, tail), :], w_sem.at[3]),
        pltpu.make_async_copy(wd_hbm, wd.at[pl.ds(0, hid), :], w_sem.at[4]),
    ]
    for copy in w_copies:
        copy.start()
    x_copy(0, 1, 0).start()
    res_copy = pltpu.make_async_copy(res_hbm, res, res_sem)
    res_copy.start()

    barrier = pltpu.get_barrier_semaphore()
    for peer in (partner, ahead, behind):
        pl.semaphore_signal(barrier, inc=1, device_id={"tp": peer}, device_id_type=MESH)
    pl.semaphore_wait(barrier, 3)

    pad = jnp.zeros((LANE - tail, width), wd.dtype)
    wt[pl.ds(tail, LANE - tail), :] = pad
    wt[pl.ds(LANE + tail, LANE - tail), :] = pad
    wd[pl.ds(hid, LANE - tail), :] = pad
    rrecv[sends] = jnp.zeros(rrecv.shape[1:], rrecv.dtype)
    for copy in w_copies:
        copy.wait()

    def gated(gate_val, up_val):
        return (jax.nn.silu(gate_val) * up_val).astype(jnp.bfloat16)

    def hidden(x_ref):
        x = x_ref[...]
        for c in range(0, main, 256):
            gate_val = dot_nt(x, wg[c:c + 256, :])
            up_val = dot_nt(x, wu[c:c + 256, :])
            gbuf[:, c:c + 256] = gated(gate_val, up_val)
        both = dot_nt(x, wt[...])
        gbuf[:, main:main + LANE] = gated(both[:, :LANE], both[:, LANE:])

    def down(c, n):
        y = jnp.dot(gbuf[...], wd[:, c:c + n], preferred_element_type=jnp.float32)
        return y.astype(jnp.bfloat16)

    def d2d_copy(t):
        slot = lax.rem(t, 2)
        return pltpu.make_async_remote_copy(
            src_ref=dsend.at[slot], dst_ref=drecv.at[t], send_sem=ds_sem.at[slot], recv_sem=dr_sem.at[t],
            device_id={"tp": partner}, device_id_type=MESH,
        )

    def ring_copy(t):
        return pltpu.make_async_remote_copy(
            src_ref=drecv.at[t], dst_ref=rrecv.at[t], send_sem=rs_sem.at[t], recv_sem=rr_sem.at[t],
            device_id={"tp": ahead}, device_id_type=MESH,
        )

    step_n = 512

    def for_partner(t, slot):
        x_copy(t, 0, slot).wait()

        @pl.when(t >= 2)
        def _():
            d2d_copy(t).wait_send()

        hidden(xbuf.at[slot, 0])
        out = dsend.at[lax.rem(t, 2)]
        for c in range(0, width, step_n):
            out[:, c:c + step_n] = down(c, step_n)
        d2d_copy(t).start()

    def prefetch(t, slot):
        @pl.when(t + 1 < total)
        def _():
            x_copy(t + 1, 0, 1 - slot).start()
            x_copy(t + 1, 1, 1 - slot).start()

    def send_step(t, carry):
        slot = lax.rem(t, 2)
        prefetch(t, slot)
        for_partner(t, slot)
        x_copy(t, 1, slot).wait()
        hidden(xbuf.at[slot, 1])
        d2d_copy(t).wait_recv()

        @pl.when(t >= subs)
        def _():
            ring_copy(t - subs).wait_recv()

        older = jnp.where(t >= subs, t - subs, sends)
        for c in range(0, width, step_n):
            own = down(c, step_n).astype(jnp.float32)
            both = own + drecv[t, :, c:c + step_n].astype(jnp.float32)
            both = both + rrecv[older, :, c:c + step_n].astype(jnp.float32)
            drecv[t, :, c:c + step_n] = both.astype(jnp.bfloat16)
        ring_copy(t).start()
        return carry

    def last_step(t, carry):
        slot = lax.rem(t, 2)
        j = t - sends
        prefetch(t, slot)
        for_partner(t, slot)
        x_copy(t, 1, slot).wait()
        hidden(xbuf.at[slot, 1])
        d2d_copy(t).wait_recv()
        for c in range(0, width, step_n):
            own = down(c, step_n).astype(jnp.float32)
            hsum[:, c:c + step_n] = own + drecv[t, :, c:c + step_n].astype(jnp.float32)
        ring_copy(t - subs).wait_recv()

        def finish(r, carry):
            at = pl.ds(pl.multiple_of(r * 16, 16), 16)
            h = hsum[at, :] + rrecv[t - subs, at, :].astype(jnp.float32)
            h = res[pl.ds(pl.multiple_of(j * TILE + r * 16, 16), 16), :].astype(jnp.float32) + h
            mean_sq = jnp.mean(h * h, axis=-1, keepdims=True)
            out_at = pl.ds(pl.multiple_of(j * TILE + r * 16, 16), 16)
            h_ref[out_at, :] = h.astype(jnp.bfloat16)
            n_ref[out_at, :] = (h * lax.rsqrt(mean_sq + EPS) * gain_ref[...]).astype(jnp.bfloat16)
            return carry

        lax.fori_loop(0, TILE // 16, finish, 0, unroll=4)
        return carry

    lax.fori_loop(0, sends, send_step, 0)
    res_copy.wait()
    lax.fori_loop(sends, total, last_step, 0)

    for t in (total - 2, total - 1):
        d2d_copy(t).wait_send()
    for t in range(sends):
        ring_copy(t).wait_send()


def solution(mesh):
    tp = mesh.shape["tp"]

    def local_block(x_in, w_gate, w_up, w_down, residual, norm_gain):
        rows, width = residual.shape
        hid = w_gate.shape[1]
        padded = hid // LANE * LANE + LANE
        chips, subs = tp // 2, rows // TILE
        sends, total = (chips - 1) * subs, chips * subs
        bf16 = jnp.bfloat16
        any_spec = pl.BlockSpec(memory_space=pl.ANY)
        vmem_spec = pl.BlockSpec(memory_space=pltpu.VMEM)
        out = jax.ShapeDtypeStruct((rows, width), bf16)
        flops = 6 * x_in.shape[0] * width * hid
        return pl.pallas_call(
            functools.partial(mlp_kernel, tp),
            out_shape=(out, out),
            in_specs=[any_spec] * 5 + [vmem_spec],
            out_specs=(vmem_spec, vmem_spec),
            scratch_shapes=[
                pltpu.VMEM((padded - LANE, width), bf16),
                pltpu.VMEM((padded - LANE, width), bf16),
                pltpu.VMEM((2 * LANE, width), bf16),
                pltpu.VMEM((padded, width), bf16),
                pltpu.VMEM((2, 2, TILE, width), bf16),
                pltpu.VMEM((TILE, padded), bf16),
                pltpu.VMEM((2, TILE, width), bf16),
                pltpu.VMEM((total, TILE, width), bf16),
                pltpu.VMEM((sends + 1, TILE, width), bf16),
                pltpu.VMEM((rows, width), bf16),
                pltpu.VMEM((TILE, width), jnp.float32),
                pltpu.SemaphoreType.DMA((5,)),
                pltpu.SemaphoreType.DMA((2, 2)),
                pltpu.SemaphoreType.DMA,
                pltpu.SemaphoreType.DMA((2,)),
                pltpu.SemaphoreType.DMA((total,)),
                pltpu.SemaphoreType.DMA((sends,)),
                pltpu.SemaphoreType.DMA((sends,)),
            ],
            compiler_params=pltpu.CompilerParams(
                collective_id=0, has_side_effects=True, vmem_limit_bytes=56 * 2**20,
            ),
            cost_estimate=pl.CostEstimate(flops=flops, bytes_accessed=2 * x_in.size, transcendentals=0),
        )(x_in, w_gate.T, w_up.T, w_down, residual, norm_gain.reshape(1, width))

    row_spec = P(("data", "tp"), None)
    return jax.shard_map(
        local_block,
        mesh=mesh,
        in_specs=(P("data", None), P(None, "tp"), P(None, "tp"), P("tp", None), row_spec, P(None)),
        out_specs=(row_spec, row_spec),
        check_vma=False,
    )
```

time: 428 us -> 130 us (0.30)
  blocking collectives: 285 us -> 0 us
  Pallas kernels: 0 us -> 122 us
  matrix products: 116 us -> 0 us
  other arithmetic: 24.7 us -> 0 us
  local copies, waits for them, and re-layouts: 1.68 us -> 6.88 us
    all_to_all x1 -> x0, blocking collectives: 285 us -> none  [local_block(): received = lax.all_to_all(part_prod, 'tp', 0, 0, tiled=True)]
    pallas_call x0 -> x1, Pallas kernels: none -> 122 us  [local_block(): pl.pallas_call(functools.partial(mlp_kernel, tp), out_shape=(out, out), i...]
    dot_general x3 -> x0, matrix products: 116 us -> none  [the longest x1 40.3 us: local_block(): up_val = jnp.dot(x_in, w_up, preferred_element_type=jnp.float32)]
    reduce_sum x2 -> x0, other arithmetic: 20.9 us -> none  [the longest x1 16.2 us: local_block(): jnp.sum(received.reshape(tp_size, rows, received.shape[1]), axis=0, dtype...]
where the time goes in v1:
time: 130 us; the launch traced here: 129 us
  Pallas kernels  122 us (94%)
  local copies, waits for them, and re-layouts  6.88 us (5%)
    pallas_call x1, Pallas kernels, local_block(): pl.pallas_call(functools.partial(mlp_kernel, tp), out_shape=(out, out), i...  122 us
    unnamed x4, local copies, waits for them, and re-layouts  5.59 us

profile of v1, /device:TPU:81, one launch (start us, length us, event | category | flops | bytes accessed | tf_op | source)
XLA Modules:
  0.0 129.3 jit_solution(499780154069414667)
XLA Ops:
  0.6 1.3 %reshape.7.gain_ref = f32[1,1536]{1,0:T(1,128)} reshape(f32[1536]{0:T(1024)} %param.11) | data formatting | bytes 12288 | tf_op jit(solution)/shard_map/reshape | solution.py:231
  1.9 121.8 %shard_map.77 = (bf16[1024,1536]{1,0:T(8,128)(2,1)}, bf16[1024,1536]{1,0:T(8,128)(2,1)}) custom-call(bf16[8192,1536]{1,0:T(8,128)(2,1)} %x_hbm.1, bf16[1120,1536]{1,0:T(8,128)(2,1)} %bitcast.2, bf16[1120,1536]{1,0:T(8,128)(2,1)} %bitcast.3, bf16[1120,1536]{1,0:T(8,128)(2,1)} %wd_hbm.1, bf16[1024,1536]{1,0:T(8,128)(2,1)} %res_hbm.1, f32[1,1536]{1,0:T(1,128)} %reshape.7.gain_ref), custom_call_target="tpu_custom_call" | custom-call | flops 84557168640 | bytes 25165824 | tf_op jit(solution)/shard_map/pallas_call | solution.py:202
  123.8 0.0 copy-start
  123.8 3.9 %copy.10 = bf16[1024,1536]{1,0:T(8,128)(2,1)} copy(bf16[1024,1536]{1,0:T(8,128)(2,1)} %get-tuple-element.4) | data formatting | bytes 6291456
  127.7 0.0 copy-done
  127.7 1.7 %copy.11 = bf16[1024,1536]{1,0:T(8,128)(2,1)} copy(bf16[1024,1536]{1,0:T(8,128)(2,1)S(1)} %copy-done) | data formatting | bytes 6291456
Async XLA Ops:
  123.8 3.9 %copy-start = (bf16[1024,1536]{1,0:T(8,128)(2,1)S(1)}, bf16[1024,1536]{1,0:T(8,128)(2,1)}, u32[]{:S(2)}) copy-start(bf16[1024,1536]{1,0:T(8,128)(2,1)} %get-tuple-element.5) | copy-start | bytes 9437188

commit v2 on v0

v2 whole, which is shorter than its diff:
```python
import functools

import jax
import jax.numpy as jnp
from jax import lax
from jax.experimental import pallas as pl
from jax.experimental.pallas import tpu as pltpu
from jax.sharding import PartitionSpec as P

EPS = 1e-5
MESH = pl.DeviceIdType.MESH
TILE = 128
LANE = 128
STEP = 256
COLS = 512
ROWS = 16


def dot_nt(a, b):
    return lax.dot_general(a, b, (((1,), (1,)), ((), ())), preferred_element_type=jnp.float32)


def gated(gate_val, up_val):
    return (jax.nn.silu(gate_val) * up_val).astype(jnp.bfloat16)


def mlp_kernel(
    tp, x_hbm, wg_hbm, wu_hbm, wd_hbm, res_hbm, gain_ref, h_ref, n_ref,
    wg, wu, wt, wt_t, wd, xbuf, gbuf, own, dsend, drecv, rrecv, res,
    w_sem, x_sem, res_sem, ds_sem, dr_sem, rs_sem, rr_sem,
):
    rows, width = res_hbm.shape
    hid = wg_hbm.shape[0]
    main = hid // LANE * LANE
    tail = hid - main
    chips = tp // 2
    subs = rows // TILE
    sends = (chips - 1) * subs
    total = chips * subs

    me = lax.axis_index("tp")
    chip, core = me // 2, lax.rem(me, 2)
    step_dir = 1 - 2 * core
    partner = me + step_dir
    ahead = 2 * lax.rem(chip + step_dir + chips, chips) + core
    behind = 2 * lax.rem(chip - step_dir + chips, chips) + core

    def x_copies(t, slot):
        s, j = t // subs + 1, lax.rem(t, subs)
        theirs = 2 * lax.rem(chip + s * step_dir + 2 * chips, chips) + (1 - core)
        mine = 2 * lax.rem(chip - s * step_dir + 2 * chips, chips) + core
        return [
            pltpu.make_async_copy(
                x_hbm.at[pl.ds(pl.multiple_of(dest * rows + j * TILE, TILE), TILE), :],
                xbuf.at[slot, pl.ds(i * TILE, TILE), :],
                x_sem.at[slot, i],
            )
            for i, dest in enumerate((theirs, mine))
        ]

    def d2d_copy(t):
        slot = lax.rem(t, 2)
        return pltpu.make_async_remote_copy(
            src_ref=dsend.at[slot], dst_ref=drecv.at[t], send_sem=ds_sem.at[slot], recv_sem=dr_sem.at[t],
            device_id={"tp": partner}, device_id_type=MESH,
        )

    def ring_copy(t):
        return pltpu.make_async_remote_copy(
            src_ref=drecv.at[t], dst_ref=rrecv.at[t], send_sem=rs_sem.at[t], recv_sem=rr_sem.at[t],
            device_id={"tp": ahead}, device_id_type=MESH,
        )

    for copy in x_copies(0, 0):
        copy.start()
    last = main // STEP
    tail_loads = [
        pltpu.make_async_copy(wg_hbm.at[pl.ds(main, tail), :], wt.at[pl.ds(0, tail), :], w_sem.at[0, last]),
        pltpu.make_async_copy(wu_hbm.at[pl.ds(main, tail), :], wt.at[pl.ds(LANE, tail), :], w_sem.at[1, last]),
    ]
    for copy in tail_loads:
        copy.start()
    up_steps = [(c, min(STEP, main - c)) for c in range(0, main, STEP)]
    gate_loads, up_loads = [], []
    for i, (c, n) in enumerate(up_steps):
        gate_loads.append(pltpu.make_async_copy(wg_hbm.at[pl.ds(c, n), :], wg.at[pl.ds(c, n), :], w_sem.at[0, i]))
        up_loads.append(pltpu.make_async_copy(wu_hbm.at[pl.ds(c, n), :], wu.at[pl.ds(c, n), :], w_sem.at[1, i]))
    down_loads = [
        pltpu.make_async_copy(wd_hbm.at[:, pl.ds(c, COLS)], wd.at[pl.ds(0, hid), pl.ds(c, COLS)], w_sem.at[2, i])
        for i, c in enumerate(range(0, width, COLS))
    ]
    res_copy = pltpu.make_async_copy(res_hbm, res, res_sem)
    half = len(up_steps) // 2
    for copy in gate_loads[:half] + up_loads[:half]:
        copy.start()

    barrier = pltpu.get_barrier_semaphore()
    for peer in (partner, ahead, behind):
        pl.semaphore_signal(barrier, inc=1, device_id={"tp": peer}, device_id_type=MESH)

    pad = jnp.zeros((LANE - tail, width), wd.dtype)
    wt[pl.ds(tail, LANE - tail), :] = pad
    wt[pl.ds(LANE + tail, LANE - tail), :] = pad
    wd[pl.ds(hid, LANE - tail), :] = pad

    def hidden_step(t, c, n):
        x = xbuf[lax.rem(t, 2)]
        gbuf[lax.rem(t, 2), :, c:c + n] = gated(dot_nt(x, wg[c:c + n, :]), dot_nt(x, wu[c:c + n, :]))

    def hidden_tail(t):
        for i in range(2):
            at = pl.ds(i * TILE, TILE)
            both = jnp.dot(xbuf[lax.rem(t, 2), at, :], wt_t[...], preferred_element_type=jnp.float32)
            gbuf[lax.rem(t, 2), at, main:main + LANE] = gated(both[:, :LANE], both[:, LANE:])

    def down_step(t, c):
        g = gbuf[lax.rem(t, 2)]
        y = jnp.dot(g, wd[:, c:c + COLS], preferred_element_type=jnp.float32).astype(jnp.bfloat16)
        dsend[lax.rem(t, 2), :, c:c + COLS] = y[:TILE]
        own[lax.rem(t, subs), :, c:c + COLS] = y[TILE:]

    def down_rows(t, c, i):
        g = gbuf[lax.rem(t, 2), pl.ds(i * TILE, TILE), :]
        y = jnp.dot(g, wd[:, c:c + COLS], preferred_element_type=jnp.float32).astype(jnp.bfloat16)
        if i == 0:
            dsend[lax.rem(t, 2), :, c:c + COLS] = y
        else:
            own[lax.rem(t, subs), :, c:c + COLS] = y

    def combine(t, first, part=0, parts=1):
        for r in range(part * TILE // parts, (part + 1) * TILE // parts, ROWS):
            for c in range(0, width, COLS):
                at = (pl.ds(r, ROWS), slice(c, c + COLS))
                both = own[lax.rem(t, subs), *at].astype(jnp.float32) + drecv[t, *at].astype(jnp.float32)
                if not first:
                    both = both + rrecv[t - subs, *at].astype(jnp.float32)
                drecv[t, *at] = both.astype(jnp.bfloat16)

    def finish_rows(j, r):
        at = pl.ds(r, ROWS)
        out_at = pl.ds(pl.multiple_of(j * TILE + r, ROWS), ROWS)
        y = own[j, at, :].astype(jnp.float32) + drecv[sends + j, at, :].astype(jnp.float32)
        y = y + rrecv[sends - subs + j, at, :].astype(jnp.float32)
        h = res[out_at, :].astype(jnp.float32) + y
        mean_sq = jnp.mean(h * h, axis=-1, keepdims=True)
        h_ref[out_at, :] = h.astype(jnp.bfloat16)
        n_ref[out_at, :] = (h * lax.rsqrt(mean_sq + EPS) * gain_ref[...].reshape(1, width)).astype(jnp.bfloat16)

    def wait_last(j):
        d2d_copy(sends + j).wait_recv()
        ring_copy(sends - subs + j).wait_recv()

    def early_tile(t, with_sum=True):
        for copy in x_copies(t + 2, lax.rem(t, 2)):
            copy.start()
        for copy in x_copies(t + 1, lax.rem(t + 1, 2)):
            copy.wait()

        if with_sum:
            d2d_copy(t).wait_send()
        if with_sum:
            d2d_copy(t - 1).wait_recv()
            combine(t - 1, True)
            ring_copy(t - 1).start()
        for c in range(0, width, COLS):
            down_step(t, c)
        d2d_copy(t).start()
        for c, n in up_steps:
            hidden_step(t + 1, c, n)
        hidden_tail(t + 1)

    def tile(t, with_sum, with_end):
        @pl.when(t + 2 < total)
        def _():
            for copy in x_copies(t + 2, lax.rem(t, 2)):
                copy.start()

        for copy in x_copies(t + 1, lax.rem(t + 1, 2)):
            copy.wait()
        d2d_copy(t).wait_send()
        if with_sum:
            d2d_copy(t - 2).wait_recv()
            ring_copy(t - 2 - subs).wait_recv()
        if with_end:
            wait_last(t - 2 - sends)
        for c in range(0, width, COLS):
            down_step(t, c)
        parts = len(up_steps)
        for i, (c, n) in enumerate(up_steps):
            hidden_step(t + 1, c, n)
            if with_sum:
                combine(t - 2, False, i, parts)
            if with_end:
                for r in range(i * TILE // parts, (i + 1) * TILE // parts, ROWS):
                    finish_rows(t - 2 - sends, r)
        hidden_tail(t + 1)
        if with_sum:
            ring_copy(t - 2).start()
        d2d_copy(t).start()

    for copy in x_copies(0, 0):
        copy.wait()
    for copy in tail_loads:
        copy.wait()
    for copy in gate_loads[half:] + up_loads[half:]:
        copy.start()
    wt_t[...] = wt[...].T
    hidden_tail(0)
    for part in (range(half), range(half, len(up_steps))):
        for i in part:
            gate_loads[i].wait()
            up_loads[i].wait()
        if not part[0]:
            for copy in down_loads:
                copy.start()
        for i in part:
            hidden_step(0, *up_steps[i])
    for copy in x_copies(1, 1):
        copy.start()
    for copy in down_loads:
        copy.wait()
    pl.semaphore_wait(barrier, 3)
    for c in range(0, width, COLS):
        down_rows(0, c, 0)
    d2d_copy(0).start()
    for copy in x_copies(2, 0):
        copy.start()
    for copy in x_copies(1, 1):
        copy.wait()
    for c in range(0, width, COLS):
        down_rows(0, c, 1)
    for c, n in up_steps[:half]:
        hidden_step(1, c, n)
    res_copy.start()
    d2d_copy(0).wait_recv()
    combine(0, True)
    ring_copy(0).start()
    for c, n in up_steps[half:]:
        hidden_step(1, c, n)
    hidden_tail(1)

    def early(t, carry):
        early_tile(t)
        return carry

    def with_sum(t, carry):
        tile(t, True, False)
        return carry

    def with_end(t, carry):
        tile(t, False, True)
        return carry

    early_tile(1, False)
    lax.fori_loop(2, subs + 1, early, 0)
    tile(subs + 1, False, False)
    lax.fori_loop(subs + 2, sends + 2, with_sum, 0)
    res_copy.wait()
    lax.fori_loop(sends + 2, total - 1, with_end, 0)
    d2d_copy(total - 1).wait_send()
    for c in range(0, width, COLS):
        down_step(total - 1, c)
    d2d_copy(total - 1).start()

    def finish_tile(j, carry):
        wait_last(j)
        for r in range(0, TILE, ROWS):
            finish_rows(j, r)
        return carry

    lax.fori_loop(total - 3 - sends, subs, finish_tile, 0)

    for t in (total - 2, total - 1):
        d2d_copy(t).wait_send()
    for t in range(sends):
        ring_copy(t).wait_send()


def store_kernel(h_ref, n_ref, h_hbm, n_hbm, sem):
    rows = h_ref.shape[0] // 4
    copies = [
        pltpu.make_async_copy(src.at[pl.ds(i * rows, rows), :], dst.at[pl.ds(i * rows, rows), :], sem.at[k, i])
        for i in range(4)
        for k, (src, dst) in enumerate(((h_ref, h_hbm), (n_ref, n_hbm)))
    ]
    for copy in copies:
        copy.start()
    for copy in copies:
        copy.wait()


def solution(mesh):
    tp = mesh.shape["tp"]

    def local_block(x_in, w_gate, w_up, w_down, residual, norm_gain):
        rows, width = residual.shape
        hid = w_gate.shape[1]
        main = hid // LANE * LANE
        padded = main + LANE
        chips, subs = tp // 2, rows // TILE
        sends, total = (chips - 1) * subs, chips * subs
        bf16 = jnp.bfloat16
        any_spec = pl.BlockSpec(memory_space=pl.ANY)
        vmem_spec = pl.BlockSpec(memory_space=pltpu.VMEM)
        out = pltpu.VMEM((rows, width), bf16)
        flops = 6 * x_in.shape[0] * width * hid
        h_out, n_out = pl.pallas_call(
            functools.partial(mlp_kernel, tp),
            out_shape=(out, out),
            in_specs=[any_spec] * 5 + [vmem_spec],
            out_specs=(vmem_spec, vmem_spec),
            scratch_shapes=[
                pltpu.VMEM((main, width), bf16),
                pltpu.VMEM((main, width), bf16),
                pltpu.VMEM((2 * LANE, width), bf16),
                pltpu.VMEM((width, 2 * LANE), bf16),
                pltpu.VMEM((padded, width), bf16),
                pltpu.VMEM((2, 2 * TILE, width), bf16),
                pltpu.VMEM((2, 2 * TILE, padded), bf16),
                pltpu.VMEM((subs, TILE, width), bf16),
                pltpu.VMEM((2, TILE, width), bf16),
                pltpu.VMEM((total, TILE, width), bf16),
                pltpu.VMEM((sends, TILE, width), bf16),
                pltpu.VMEM((rows, width), bf16),
                pltpu.SemaphoreType.DMA((3, main // STEP + 2)),
                pltpu.SemaphoreType.DMA((2, 2)),
                pltpu.SemaphoreType.DMA,
                pltpu.SemaphoreType.DMA((2,)),
                pltpu.SemaphoreType.DMA((total,)),
                pltpu.SemaphoreType.DMA((sends,)),
                pltpu.SemaphoreType.DMA((sends,)),
            ],
            compiler_params=pltpu.CompilerParams(
                collective_id=0, has_side_effects=True, vmem_limit_bytes=56 * 2**20,
            ),
            cost_estimate=pl.CostEstimate(flops=flops, bytes_accessed=2 * x_in.size, transcendentals=0),
        )(x_in, w_gate.T, w_up.T, w_down, residual, norm_gain)
        stored = jax.ShapeDtypeStruct((rows, width), bf16)
        return pl.pallas_call(
            store_kernel,
            out_shape=(stored, stored),
            in_specs=[vmem_spec, vmem_spec],
            out_specs=(any_spec, any_spec),
            scratch_shapes=[pltpu.SemaphoreType.DMA((2, 4))],
            compiler_params=pltpu.CompilerParams(vmem_limit_bytes=2**20),
        )(pltpu.with_memory_space_constraint(h_out, pltpu.VMEM), pltpu.with_memory_space_constraint(n_out, pltpu.VMEM))

    row_spec = P(("data", "tp"), None)
    return jax.shard_map(
        local_block,
        mesh=mesh,
        in_specs=(P("data", None), P(None, "tp"), P(None, "tp"), P("tp", None), row_spec, P(None)),
        out_specs=(row_spec, row_spec),
        check_vma=False,
    )
```

time: 428 us -> 120 us (0.28)
  blocking collectives: 285 us -> 0 us
  Pallas kernels: 0 us -> 118 us
  matrix products: 116 us -> 0 us
  other arithmetic: 24.7 us -> 0 us
    all_to_all x1 -> x0, blocking collectives: 285 us -> none  [local_block(): received = lax.all_to_all(part_prod, 'tp', 0, 0, tiled=True)]
    pallas_call x0 -> x2, Pallas kernels: none -> 118 us  [the longest x1 115 us: local_block(): pl.pallas_call(functools.partial(mlp_kernel, tp), out_shape=(out, out), i...]
    dot_general x3 -> x0, matrix products: 116 us -> none  [the longest x1 40.3 us: local_block(): up_val = jnp.dot(x_in, w_up, preferred_element_type=jnp.float32)]
    reduce_sum x2 -> x0, other arithmetic: 20.9 us -> none  [the longest x1 16.2 us: local_block(): jnp.sum(received.reshape(tp_size, rows, received.shape[1]), axis=0, dtype...]
where the time goes in v2:
time: 120 us; the launch traced here: 119 us
  Pallas kernels  118 us (98%)
    pallas_call x1, Pallas kernels, local_block(): pl.pallas_call(functools.partial(mlp_kernel, tp), out_shape=(out, out), i...  115 us
    pallas_call x1, Pallas kernels, local_block(): pl.pallas_call(store_kernel, out_shape=(stored, stored), in_specs=[vmem_s...  2.74 us

profile of v2, /device:TPU:81, one launch (start us, length us, event | category | flops | bytes accessed | tf_op | source)
XLA Modules:
  0.0 118.6 jit_solution(7860922312897638074)
XLA Ops:
  0.6 115.0 %shard_map.77 = (bf16[1024,1536]{1,0:T(8,128)(2,1)S(1)}, bf16[1024,1536]{1,0:T(8,128)(2,1)S(1)}) custom-call(bf16[8192,1536]{1,0:T(8,128)(2,1)} %x_hbm.1, bf16[1120,1536]{1,0:T(8,128)(2,1)} %bitcast.2, bf16[1120,1536]{1,0:T(8,128)(2,1)} %bitcast.3, bf16[1120,1536]{1,0:T(8,128)(2,1)} %wd_hbm.1, bf16[1024,1536]{1,0:T(8,128)(2,1)} %res_hbm.1, f32[1536]{0:T(1024)} %gain_ref.1), custom_call_target="tpu_custom_call" | custom-call | flops 84557168640 | bytes 25165824 | tf_op jit(solution)/shard_map/pallas_call | solution.py:307
  115.7 2.7 %shard_map.78 = (bf16[1024,1536]{1,0:T(8,128)(2,1)}, bf16[1024,1536]{1,0:T(8,128)(2,1)}) custom-call(bf16[1024,1536]{1,0:T(8,128)(2,1)S(1)} %get-tuple-element.4.h_ref, bf16[1024,1536]{1,0:T(8,128)(2,1)S(1)} %get-tuple-element.5.n_ref), custom_call_target="tpu_custom_call" | custom-call | tf_op jit(solution)/shard_map/pallas_call | solution.py:339

commit v3 on v2

--- a/solution.py
+++ b/solution.py
@@ -85,10 +85,7 @@
     for i, (c, n) in enumerate(up_steps):
         gate_loads.append(pltpu.make_async_copy(wg_hbm.at[pl.ds(c, n), :], wg.at[pl.ds(c, n), :], w_sem.at[0, i]))
         up_loads.append(pltpu.make_async_copy(wu_hbm.at[pl.ds(c, n), :], wu.at[pl.ds(c, n), :], w_sem.at[1, i]))
-    down_loads = [
-        pltpu.make_async_copy(wd_hbm.at[:, pl.ds(c, COLS)], wd.at[pl.ds(0, hid), pl.ds(c, COLS)], w_sem.at[2, i])
-        for i, c in enumerate(range(0, width, COLS))
-    ]
+    down_loads = [pltpu.make_async_copy(wd_hbm, wd.at[pl.ds(0, hid), :], w_sem.at[2, 0])]
     res_copy = pltpu.make_async_copy(res_hbm, res, res_sem)
     half = len(up_steps) // 2
     for copy in gate_loads[:half] + up_loads[:half]:
@@ -156,8 +153,7 @@
         for copy in x_copies(t + 1, lax.rem(t + 1, 2)):
             copy.wait()
 
-        if with_sum:
-            d2d_copy(t).wait_send()
+        d2d_copy(t).wait_send()
         if with_sum:
             d2d_copy(t - 1).wait_recv()
             combine(t - 1, True)
@@ -169,7 +165,7 @@
             hidden_step(t + 1, c, n)
         hidden_tail(t + 1)
 
-    def tile(t, with_sum, with_end):
+    def tile(t, with_sum, with_end, lag=2):
         @pl.when(t + 2 < total)
         def _():
             for copy in x_copies(t + 2, lax.rem(t, 2)):
@@ -179,8 +175,8 @@
             copy.wait()
         d2d_copy(t).wait_send()
         if with_sum:
-            d2d_copy(t - 2).wait_recv()
-            ring_copy(t - 2 - subs).wait_recv()
+            d2d_copy(t - lag).wait_recv()
+            ring_copy(t - lag - subs).wait_recv()
         if with_end:
             wait_last(t - 2 - sends)
         for c in range(0, width, COLS):
@@ -189,20 +185,20 @@
         for i, (c, n) in enumerate(up_steps):
             hidden_step(t + 1, c, n)
             if with_sum:
-                combine(t - 2, False, i, parts)
+                combine(t - lag, False, i, parts)
             if with_end:
                 for r in range(i * TILE // parts, (i + 1) * TILE // parts, ROWS):
                     finish_rows(t - 2 - sends, r)
         hidden_tail(t + 1)
         if with_sum:
-            ring_copy(t - 2).start()
+            ring_copy(t - lag).start()
         d2d_copy(t).start()
 
     for copy in x_copies(0, 0):
         copy.wait()
     for copy in tail_loads:
         copy.wait()
-    for copy in gate_loads[half:] + up_loads[half:]:
+    for copy in gate_loads[half:] + up_loads[half:] + down_loads:
         copy.start()
     wt_t[...] = wt[...].T
     hidden_tail(0)
@@ -210,9 +206,6 @@
         for i in part:
             gate_loads[i].wait()
             up_loads[i].wait()
-        if not part[0]:
-            for copy in down_loads:
-                copy.start()
         for i in part:
             hidden_step(0, *up_steps[i])
     for copy in x_copies(1, 1):
@@ -251,10 +244,28 @@
         tile(t, False, True)
         return carry
 
-    early_tile(1, False)
-    lax.fori_loop(2, subs + 1, early, 0)
-    tile(subs + 1, False, False)
-    lax.fori_loop(subs + 2, sends + 2, with_sum, 0)
+    for copy in x_copies(3, 1):
+        copy.start()
+    for copy in x_copies(2, 0):
+        copy.wait()
+    for c in range(0, width, COLS):
+        down_rows(1, c, 0)
+    d2d_copy(1).start()
+    for c in range(0, width, COLS):
+        down_rows(1, c, 1)
+    for c, n in up_steps[:half]:
+        hidden_step(2, c, n)
+    d2d_copy(1).wait_recv()
+    combine(1, True)
+    ring_copy(1).start()
+    for c, n in up_steps[half:]:
+        hidden_step(2, c, n)
+    hidden_tail(2)
+    early_tile(2, False)
+    lax.fori_loop(3, subs + 1, early, 0)
+    tile(subs + 1, True, False, lag=1)
+    tile(subs + 2, False, False)
+    lax.fori_loop(subs + 3, sends + 2, with_sum, 0)
     res_copy.wait()
     lax.fori_loop(sends + 2, total - 1, with_end, 0)
     d2d_copy(total - 1).wait_send()
@@ -277,10 +288,10 @@
 
 
 def store_kernel(h_ref, n_ref, h_hbm, n_hbm, sem):
-    rows = h_ref.shape[0] // 4
+    rows = h_ref.shape[0] // 2
     copies = [
         pltpu.make_async_copy(src.at[pl.ds(i * rows, rows), :], dst.at[pl.ds(i * rows, rows), :], sem.at[k, i])
-        for i in range(4)
+        for i in range(2)
         for k, (src, dst) in enumerate(((h_ref, h_hbm), (n_ref, n_hbm)))
     ]
     for copy in copies:
@@ -341,7 +352,7 @@
             out_shape=(stored, stored),
             in_specs=[vmem_spec, vmem_spec],
             out_specs=(any_spec, any_spec),
-            scratch_shapes=[pltpu.SemaphoreType.DMA((2, 4))],
+            scratch_shapes=[pltpu.SemaphoreType.DMA((2, 2))],
             compiler_params=pltpu.CompilerParams(vmem_limit_bytes=2**20),
         )(pltpu.with_memory_space_constraint(h_out, pltpu.VMEM), pltpu.with_memory_space_constraint(n_out, pltpu.VMEM))
 

time: 120 us -> 119 us (level)
  no operation moved by 1% of the time
where the time goes in v3:
time: 119 us; the launch traced here: 118 us
  Pallas kernels  117 us (98%)
    pallas_call x1, Pallas kernels, local_block(): pl.pallas_call(functools.partial(mlp_kernel, tp), out_shape=(out, out), i...  114 us
    pallas_call x1, Pallas kernels, local_block(): pl.pallas_call(store_kernel, out_shape=(stored, stored), in_specs=[vmem_s...  2.73 us

profile of v3, /device:TPU:81, one launch (start us, length us, event | category | flops | bytes accessed | tf_op | source)
XLA Modules:
  0.0 118.0 jit_solution(4989446125688703741)
XLA Ops:
  0.6 114.5 %shard_map.77 = (bf16[1024,1536]{1,0:T(8,128)(2,1)S(1)}, bf16[1024,1536]{1,0:T(8,128)(2,1)S(1)}) custom-call(bf16[8192,1536]{1,0:T(8,128)(2,1)} %x_hbm.1, bf16[1120,1536]{1,0:T(8,128)(2,1)} %bitcast.2, bf16[1120,1536]{1,0:T(8,128)(2,1)} %bitcast.3, bf16[1120,1536]{1,0:T(8,128)(2,1)} %wd_hbm.1, bf16[1024,1536]{1,0:T(8,128)(2,1)} %res_hbm.1, f32[1536]{0:T(1024)} %gain_ref.1), custom_call_target="tpu_custom_call" | custom-call | flops 84557168640 | bytes 25165824 | tf_op jit(solution)/shard_map/pallas_call | solution.py:318
  115.1 2.7 %shard_map.78 = (bf16[1024,1536]{1,0:T(8,128)(2,1)}, bf16[1024,1536]{1,0:T(8,128)(2,1)}) custom-call(bf16[1024,1536]{1,0:T(8,128)(2,1)S(1)} %get-tuple-element.4.h_ref, bf16[1024,1536]{1,0:T(8,128)(2,1)S(1)} %get-tuple-element.5.n_ref), custom_call_target="tpu_custom_call" | custom-call | tf_op jit(solution)/shard_map/pallas_call | solution.py:350

commit v4 on v3

--- a/solution.py
+++ b/solution.py
@@ -196,10 +196,10 @@
 
     for copy in x_copies(0, 0):
         copy.wait()
+    for copy in gate_loads[half:] + up_loads[half:] + down_loads:
+        copy.start()
     for copy in tail_loads:
         copy.wait()
-    for copy in gate_loads[half:] + up_loads[half:] + down_loads:
-        copy.start()
     wt_t[...] = wt[...].T
     hidden_tail(0)
     for part in (range(half), range(half, len(up_steps))):

time: 119 us -> 119 us (level)
  no operation moved by 1% of the time
where the time goes in v4:
time: 119 us; the launch traced here: 118 us
  Pallas kernels  117 us (98%)
    pallas_call x1, Pallas kernels, local_block(): pl.pallas_call(functools.partial(mlp_kernel, tp), out_shape=(out, out), i...  114 us
    pallas_call x1, Pallas kernels, local_block(): pl.pallas_call(store_kernel, out_shape=(stored, stored), in_specs=[vmem_s...  2.73 us

profile of v4, /device:TPU:81, one launch (start us, length us, event | category | flops | bytes accessed | tf_op | source)
XLA Modules:
  0.0 118.0 jit_solution(17095097728177604067)
XLA Ops:
  0.6 114.5 %shard_map.77 = (bf16[1024,1536]{1,0:T(8,128)(2,1)S(1)}, bf16[1024,1536]{1,0:T(8,128)(2,1)S(1)}) custom-call(bf16[8192,1536]{1,0:T(8,128)(2,1)} %x_hbm.1, bf16[1120,1536]{1,0:T(8,128)(2,1)} %bitcast.2, bf16[1120,1536]{1,0:T(8,128)(2,1)} %bitcast.3, bf16[1120,1536]{1,0:T(8,128)(2,1)} %wd_hbm.1, bf16[1024,1536]{1,0:T(8,128)(2,1)} %res_hbm.1, f32[1536]{0:T(1024)} %gain_ref.1), custom_call_target="tpu_custom_call" | custom-call | flops 84557168640 | bytes 25165824 | tf_op jit(solution)/shard_map/pallas_call | solution.py:318
  115.1 2.7 %shard_map.78 = (bf16[1024,1536]{1,0:T(8,128)(2,1)}, bf16[1024,1536]{1,0:T(8,128)(2,1)}) custom-call(bf16[1024,1536]{1,0:T(8,128)(2,1)S(1)} %get-tuple-element.4.h_ref, bf16[1024,1536]{1,0:T(8,128)(2,1)S(1)} %get-tuple-element.5.n_ref), custom_call_target="tpu_custom_call" | custom-call | tf_op jit(solution)/shard_map/pallas_call | solution.py:350
